TPU v7x, 32 devices: a whole 2x2x4 slice. The times are simulated.
32 devices in a mesh: gx: 4 (over y, x), gy: 8 (over z, core).
Axes of the slice: x: 2, y: 2, z: 4, core: 2. Of those that a mesh axis runs over, the one named last changes fastest.
Arguments:
- sources: bfloat16 [1024, 64, 512], P(('gx', 'gy')), may hold values from -6 to 6
- projection: bfloat16 [512, 512], replicated, may hold values from -0.25 to 0.25
- translations: bfloat16 [5, 2, 512, 512], replicated, may hold values from -0.1875 to 0.1875
- angles: float32 [6, 1024, 256], P(None, ('gx', 'gy')), may hold values from -3.140625 to 3.140625
- interpolation: bfloat16 [256, 1024], replicated, may hold values from -0.25 to 0.25
- box_order: int32 [1024], P(('gx', 'gy')), may hold values from 0 to 1023, as said below
Outputs:
- targets: bfloat16 [1024, 128, 512], P(('gx', 'gy'))
Inputs may be any that keep to these rules, and one draw needn't show every extreme that they name: `box_order`: each aligned block of 32 entries (entries k * 32 to (k + 1) * 32 - 1) is a permutation of those same indices.
All inputs are finite; a program needn't handle non-finite values.
Results may differ from a plain program's by a relative error of at most 0.014.
Values may be sent and summed in bfloat16 or wider, within the bound.
A program may use at most 64 MiB of HBM per device.

v0:
```python
import jax
import jax.numpy as jnp
from jax import lax
from jax.sharding import PartitionSpec as P


def swapped(value, axis, apart):
    mask = 2**apart
    pairs = [(source, source ^ mask) for source in range(lax.axis_size(axis))]
    return lax.ppermute(value, axis, pairs)


def mix_parts(product, coeffs, sides):
    first_part = product[..., :coeffs]
    second_part = product[..., coeffs:]
    real_part = first_part[..., :sides, :] - second_part[..., sides:, :]
    imag_part = first_part[..., sides:, :] + second_part[..., :sides, :]
    return (real_part, imag_part)


def rotate(real_part, imag_part, angle_row):
    cosine = jnp.cos(angle_row)[..., None, :]
    sine_part = jnp.sin(angle_row)[..., None, :]
    return jnp.concatenate(
        [cosine * real_part - sine_part * imag_part, sine_part * real_part + cosine * imag_part],
        axis=-2,
    )


def level_plan(count_x, count_y):
    bits_x = count_x.bit_length() - 1
    bits_y = count_y.bit_length() - 1
    return [
        ("gy", bits_y - 1),
        ("gx", bits_x - 1),
        ("gy", bits_y - 2),
        ("gx", bits_x - 2),
        ("gy", bits_y - 3),
    ]


def interpolate(coeff_state, interpolation, sides, points):
    product = jnp.einsum(
        "bck,kq->bcq", coeff_state, interpolation, preferred_element_type=jnp.float32
    )
    real_part = product[:, :sides, :points] - product[:, sides:, points:]
    imag_part = product[:, :sides, points:] + product[:, sides:, :points]
    return jnp.concatenate([real_part, imag_part], axis=1).astype(jnp.bfloat16)


def level_step(coeff_state, level_weights, angle_row, bit_pos, coeffs, sides):
    half_bit = lax.axis_index("gx") >> bit_pos & 1
    weight = lax.dynamic_index_in_dim(level_weights, half_bit, 0, keepdims=False)
    partner = swapped(coeff_state, "gx", bit_pos)
    joined = jnp.where(
        half_bit == 0,
        jnp.concatenate([coeff_state, partner], axis=-1),
        jnp.concatenate([partner, coeff_state], axis=-1),
    )
    product = jnp.einsum("bck,kq->bcq", joined, weight, preferred_element_type=jnp.float32)
    real_part, imag_part = mix_parts(product, coeffs, sides)
    return rotate(real_part, imag_part, angle_row).astype(jnp.bfloat16)


def local_pair_step(coeff_state, level_weights, angle_row, bit_pos, count_y, coeffs, sides):
    stride = 1 << bit_pos
    box_count = coeff_state.shape[0]
    per_peer = box_count // count_y
    groups = count_y // (2 * stride)
    grouped = coeff_state.reshape((groups, 2, stride * per_peer) + coeff_state.shape[1:])
    angle_grouped = angle_row.reshape(groups, 2, stride * per_peer, angle_row.shape[-1])
    joined = jnp.concatenate([grouped[:, 0], grouped[:, 1]], axis=-1)
    halves = []
    for half_bit in range(2):
        product = jnp.einsum(
            "gbck,kq->gbcq", joined, level_weights[half_bit], preferred_element_type=jnp.float32
        )
        real_part, imag_part = mix_parts(product, coeffs, sides)
        halves.append(rotate(real_part, imag_part, angle_grouped[:, half_bit]).astype(jnp.bfloat16))
    return jnp.stack(halves, axis=1).reshape(coeff_state.shape)


def local(sources, projection, translations, angles, interpolation, box_order):
    box_count, sides, points = sources.shape
    coeffs = projection.shape[1] // 2
    product = jnp.einsum("brp,pk->brk", sources, projection, preferred_element_type=jnp.float32)
    stacked = jnp.concatenate([product[..., :coeffs], product[..., coeffs:]], axis=1)
    local_slot = box_order % box_count
    onehot = (local_slot[None, :] == jnp.arange(box_count, dtype=jnp.int32)[:, None]).astype(
        jnp.float32
    )
    placed = jnp.einsum("ji,ick->jck", onehot, stacked, precision=lax.Precision.HIGHEST)
    coeff_state = rotate(placed[:, :sides], placed[:, sides:], angles[0]).astype(jnp.bfloat16)
    plan = level_plan(lax.axis_size("gx"), lax.axis_size("gy"))
    later_angles = jnp.moveaxis(angles[1:], 0, 1)
    wide_state, later_angles = (
        lax.all_to_all(
            coeff_state.astype(jnp.float32), "gy", split_axis=0, concat_axis=0, tiled=True
        ),
        lax.all_to_all(later_angles, "gy", split_axis=0, concat_axis=0, tiled=True),
    )
    coeff_state = wide_state.astype(jnp.bfloat16)
    for level_no, (axis_name, bit_pos) in enumerate(plan):
        angle_row = later_angles[:, level_no]
        if axis_name == "gy":
            coeff_state = local_pair_step(
                coeff_state,
                translations[level_no],
                angle_row,
                bit_pos,
                lax.axis_size("gy"),
                coeffs,
                sides,
            )
        else:
            coeff_state = level_step(
                coeff_state, translations[level_no], angle_row, bit_pos, coeffs, sides
            )
    return interpolate(coeff_state, interpolation, sides, points)


def solution(mesh):
    placed = (
        P(("gx", "gy"), None, None),
        P(),
        P(),
        P(None, ("gx", "gy"), None),
        P(),
        P(("gx", "gy")),
    )
    return jax.shard_map(
        local, mesh=mesh, in_specs=placed, out_specs=P(("gx", "gy"), None, None), check_vma=False
    )
```

profile of v0, /device:TPU:0, one launch (start us, length us, event | category | flops | bytes accessed | tf_op | source)
XLA Modules:
  0.0 207.3 jit_solution(7954853428592408840)
XLA Ops:
  0.0 1.1 slice.264
  1.1 0.8 copy.80
  1.9 6.4 %all-to-all-start = ((f32[32,5,256]{2,1,0:T(8,128)}), f32[32,5,256]{2,1,0:T(8,128)S(1)}, u32[]{:S(2)}, u32[]{:S(2)}) async-start(f32[32,5,256]{2,1,0:T(8,128)} %bitcast.183), calls=%async_computation | async-start | bytes 524288 | tf_op jit(solution)/shard_map/all_to_all | solution.py:100
  8.2 0.9 cosine_bitcast_fusion
  9.1 0.7 and_select_fusion
  9.8 2.3 %fusion.50 = f32[32,64,512]{2,1,0:T(8,128)S(1)} fusion(bf16[32,64,512]{2,1,0:T(8,128)(2,1)S(1)} %copy-done, bf16[512,512]{1,0:T(8,128)(2,1)} %param.7), kind=kOutput, calls=%fused_computation.107 | convolution fusion | flops 1073741824 | bytes 6815744 | tf_op jit(solution)/shard_map/brp,pk->brk/dot_general | solution.py:86
  12.8 4.9 %fusion.14 = f32[32,128,256]{2,0,1:T(8,128)S(1)} fusion(f32[32,128,256]{2,1,0:T(8,128)S(1)} %pad_maximum_fusion, s32[32]{0:T(128)S(1)} %and_select_fusion), kind=kOutput, calls=%fused_computation.20 | convolution fusion | flops 402654208 | bytes 8388736 | tf_op jit(solution)/shard_map/ji,ick->jck/dot_general | solution.py:92
  17.8 0.8 subtract_convert_fusion.2
  18.7 2.5 %copy.36 = bf16[32,128,256]{2,1,0:T(8,128)(2,1)} copy(bf16[32,128,256]{2,0,1:T(8,128)(2,1)S(1)} %maximum_convert_fusion) | data formatting | bytes 4194304 | tf_op jit(solution)/shard_map/convert_element_type | solution.py:98
  21.2 5.1 %all-to-all-start.1 = ((bf16[32,128,256]{2,1,0:T(8,128)(2,1)}), bf16[32,128,256]{2,1,0:T(8,128)(2,1)S(1)}, u32[]{:S(2)}, u32[]{:S(2)}) async-start(bf16[32,128,256]{2,1,0:T(8,128)(2,1)} %copy.36), calls=%async_computation.1 | async-start | bytes 4194304 | tf_op jit(solution)/shard_map/all_to_all | solution.py:97
  26.3 2.1 fusion.76
  28.5 46.8 %all-to-all-done.1 = bf16[32,128,256]{2,1,0:T(8,128)(2,1)S(1)} async-done(((bf16[32,128,256]{2,1,0:T(8,128)(2,1)}), bf16[32,128,256]{2,1,0:T(8,128)(2,1)S(1)}, u32[]{:S(2)}, u32[]{:S(2)}) %all-to-all-start.1) | async-done | bytes 2097184 | tf_op jit(solution)/shard_map/all_to_all | solution.py:97
  75.5 2.3 %convolution_bitcast_fusion = f32[1,16,128,512]{3,2,1,0:T(8,128)S(1)} fusion(bf16[1,16,128,256]{3,2,1,0:T(8,128)(2,1)S(1)} %get-tuple-element.34, bf16[1,16,128,256]{3,2,1,0:T(8,128)(2,1)S(1)} %get-tuple-element.33, bf16[5,2,512,512]{3,2,1,0:T(8,128)(2,1)} %param.8), kind=kOutput, calls=%fused_computation.24 | convolution fusion | flops 1077936128 | bytes 6815744 | tf_op jit(solution)/shard_map/gbck,kq->gbcq/dot_general | solution.py:75
  77.8 2.3 %convolution_bitcast_fusion.1 = f32[1,16,128,512]{3,2,1,0:T(8,128)S(1)} fusion(bf16[1,16,128,256]{3,2,1,0:T(8,128)(2,1)S(1)} %get-tuple-element.34, bf16[1,16,128,256]{3,2,1,0:T(8,128)(2,1)S(1)} %get-tuple-element.33, bf16[5,2,512,512]{3,2,1,0:T(8,128)(2,1)} %param.8), kind=kOutput, calls=%fused_computation.25 | convolution fusion | flops 1077936128 | bytes 6815744 | tf_op jit(solution)/shard_map/gbck,kq->gbcq/dot_general | solution.py:75
  81.2 1.6 collective-permute-start
  82.8 1.7 fusion.74
  84.6 43.8 %collective-permute-done = bf16[32,128,256]{2,1,0:T(8,128)(2,1)} collective-permute-done((bf16[32,128,256]{2,1,0:T(8,128)(2,1)S(1)}, bf16[32,128,256]{2,1,0:T(8,128)(2,1)}, u32[]{:S(2)}, u32[]{:S(2)}) %collective-permute-start) | collective-permute-done | bytes 2097184 | tf_op jit(solution)/shard_map/ppermute | solution.py:10
  128.5 4.2 %fusion.2 = f32[32,128,512]{2,1,0:T(8,128)S(1)} fusion(bf16[32,128,256]{2,1,0:T(8,128)(2,1)} %collective-permute-done, bf16[32,128,256]{2,1,0:T(8,128)(2,1)S(1)} %bitcast.191, pred[]{:T(512)S(6)} %eq.22, bf16[1,2,512,512]{3,2,1,0:T(8,128)(2,1)S(1)} %get-tuple-element.12, s32[]{:T(128)S(6)} %select_n.32), kind=kOutput, calls=%fused_computation.6 | convolution fusion | flops 2166358016 | bytes 13107205 | tf_op jit(solution)/shard_map/bck,kq->bcq/dot_general | solution.py:60
  132.7 1.0 subtract_convert_fusion.1
  133.9 2.3 %fusion.20 = f32[2,8,128,512]{3,2,1,0:T(8,128)S(1)} fusion(bf16[2,8,128,256]{3,2,1,0:T(8,128)(2,1)S(1)} %get-tuple-element.32, bf16[2,8,128,256]{3,2,1,0:T(8,128)(2,1)S(1)} %get-tuple-element.31, bf16[5,2,512,512]{3,2,1,0:T(8,128)(2,1)} %param.8), kind=kOutput, calls=%fused_computation.49 | convolution fusion | flops 1077936128 | bytes 6815744 | tf_op jit(solution)/shard_map/gbck,kq->gbcq/dot_general | solution.py:75
  136.2 2.3 %fusion.21 = f32[2,8,128,512]{3,2,1,0:T(8,128)S(1)} fusion(bf16[2,8,128,256]{3,2,1,0:T(8,128)(2,1)S(1)} %get-tuple-element.32, bf16[2,8,128,256]{3,2,1,0:T(8,128)(2,1)S(1)} %get-tuple-element.31, bf16[5,2,512,512]{3,2,1,0:T(8,128)(2,1)} %param.8), kind=kOutput, calls=%fused_computation.50 | convolution fusion | flops 1077936128 | bytes 6815744 | tf_op jit(solution)/shard_map/gbck,kq->gbcq/dot_general | solution.py:75
  139.6 1.5 copy.41
  141.2 1.5 collective-permute-start.1
  143.0 44.8 %collective-permute-done.1 = bf16[32,128,256]{2,1,0:T(8,128)(2,1)} collective-permute-done((bf16[32,128,256]{2,1,0:T(8,128)(2,1)}, bf16[32,128,256]{2,1,0:T(8,128)(2,1)}, u32[]{:S(2)}, u32[]{:S(2)}) %collective-permute-start.1) | collective-permute-done | bytes 2097184 | tf_op jit(solution)/shard_map/ppermute | solution.py:10
  187.7 5.1 %fusion.8 = f32[32,128,512]{2,1,0:T(8,128)S(1)} fusion(bf16[32,128,256]{2,1,0:T(8,128)(2,1)} %collective-permute-done.1, bf16[32,128,256]{2,1,0:T(8,128)(2,1)} %bitcast.46, pred[]{:T(512)S(6)} %eq.21, bf16[1,2,512,512]{3,2,1,0:T(8,128)(2,1)S(1)} %get-tuple-element.11, s32[]{:T(128)S(6)} %select_n.34), kind=kOutput, calls=%fused_computation.13 | convolution fusion | flops 2166358016 | bytes 13107205 | tf_op jit(solution)/shard_map/bck,kq->bcq/dot_general | solution.py:60
  192.8 1.0 subtract_convert_fusion
  194.0 2.3 %fusion.18 = f32[4,4,128,512]{3,2,1,0:T(8,128)S(1)} fusion(bf16[4,4,128,256]{3,2,1,0:T(8,128)(2,1)S(1)} %get-tuple-element.30, bf16[4,4,128,256]{3,2,1,0:T(8,128)(2,1)S(1)} %get-tuple-element.29, bf16[5,2,512,512]{3,2,1,0:T(8,128)(2,1)} %param.8), kind=kOutput, calls=%fused_computation.47 | convolution fusion | flops 1077936128 | bytes 6815744 | tf_op jit(solution)/shard_map/gbck,kq->gbcq/dot_general | solution.py:75
  196.3 2.3 %fusion.19 = f32[4,4,128,512]{3,2,1,0:T(8,128)S(1)} fusion(bf16[4,4,128,256]{3,2,1,0:T(8,128)(2,1)S(1)} %get-tuple-element.30, bf16[4,4,128,256]{3,2,1,0:T(8,128)(2,1)S(1)} %get-tuple-element.29, bf16[5,2,512,512]{3,2,1,0:T(8,128)(2,1)} %param.8), kind=kOutput, calls=%fused_computation.48 | convolution fusion | flops 1077936128 | bytes 6815744 | tf_op jit(solution)/shard_map/gbck,kq->gbcq/dot_general | solution.py:75
  200.0 0.8 copy-done.2
  200.8 2.3 %fusion.48 = f32[32,128,1024]{2,1,0:T(8,128)S(1)} fusion(bf16[32,128,256]{2,1,0:T(8,128)(2,1)S(1)} %bitcast.184, bf16[256,1024]{1,0:T(8,128)(2,1)S(1)} %copy-done.2), kind=kOutput, calls=%fused_computation.105 | convolution fusion | flops 2147483648 | bytes 19398656 | tf_op jit(solution)/shard_map/bck,kq->bcq/dot_general | solution.py:43
  203.2 1.7 fusion.1
  204.8 2.5 %pad_maximum_fusion.1 = bf16[32,128,512]{2,1,0:T(8,128)(2,1)} fusion(bf16[32,64,512]{2,1,0:T(8,128)(2,1)S(1)} %get-tuple-element.6, bf16[32,64,512]{2,1,0:T(8,128)(2,1)S(1)} %get-tuple-element.5), kind=kLoop, calls=%fused_computation.19 | loop fusion | flops 8388608 | bytes 8388608 | tf_op jit(solution)/shard_map/concatenate | solution.py:48
  (30 shorter events, 5.5 us)
Async XLA Ops:
  0.0 9.8 %copy-start = (bf16[32,64,512]{2,1,0:T(8,128)(2,1)S(1)}, bf16[32,64,512]{2,1,0:T(8,128)(2,1)}, u32[]{:S(2)}) copy-start(bf16[32,64,512]{2,1,0:T(8,128)(2,1)} %param.6) | copy-start | bytes 6291460
  1.9 19.3 %all-to-all-start = ((f32[32,5,256]{2,1,0:T(8,128)}), f32[32,5,256]{2,1,0:T(8,128)S(1)}, u32[]{:S(2)}, u32[]{:S(2)}) async-start(f32[32,5,256]{2,1,0:T(8,128)} %bitcast.183), calls=%async_computation | async-start | bytes 524288 | tf_op jit(solution)/shard_map/all_to_all | solution.py:100
  21.2 54.1 %all-to-all-start.1 = ((bf16[32,128,256]{2,1,0:T(8,128)(2,1)}), bf16[32,128,256]{2,1,0:T(8,128)(2,1)S(1)}, u32[]{:S(2)}, u32[]{:S(2)}) async-start(bf16[32,128,256]{2,1,0:T(8,128)(2,1)} %copy.36), calls=%async_computation.1 | async-start | bytes 4194304 | tf_op jit(solution)/shard_map/all_to_all | solution.py:97
  81.2 47.2 %collective-permute-start = (bf16[32,128,256]{2,1,0:T(8,128)(2,1)S(1)}, bf16[32,128,256]{2,1,0:T(8,128)(2,1)}, u32[]{:S(2)}, u32[]{:S(2)}) collective-permute-start(bf16[32,128,256]{2,1,0:T(8,128)(2,1)S(1)} %bitcast.190), channel_id=1, source_target_pairs={{0,16},{8,24},{16,0},{24,8},{1,17},{9,25},{17,1},{25,9},{2,18},{10... | collective-permute-start | bytes 6291464 | tf_op jit(solution)/shard_map/ppermute | solution.py:10
  141.2 46.5 %collective-permute-start.1 = (bf16[32,128,256]{2,1,0:T(8,128)(2,1)}, bf16[32,128,256]{2,1,0:T(8,128)(2,1)}, u32[]{:S(2)}, u32[]{:S(2)}) collective-permute-start(bf16[32,128,256]{2,1,0:T(8,128)(2,1)} %bitcast.46), channel_id=1, source_target_pairs={{0,8},{8,0},{16,24},{24,16},{1,9},{9,1},{17,25},{25,17},{2,10},{10... | collective-permute-start | bytes 6291464 | tf_op jit(solution)/shard_map/ppermute | solution.py:10
  199.8 1.0 copy-start.2
  204.8 2.5 %copy-start.1 = (bf16[32,64,512]{2,1,0:T(8,128)(2,1)S(1)}, bf16[32,64,512]{2,1,0:T(8,128)(2,1)}, u32[]{:S(2)}) copy-start(bf16[32,64,512]{2,1,0:T(8,128)(2,1)} %param.6) | copy-start | bytes 6291460
where the time goes:
time: 208 us; the launch traced here: 207 us
  waiting for transfers between devices  135 us (65%)
  matrix products  32.6 us (16%)
  starting transfers between devices  14.5 us (7%)
  local copies, waits for them, and re-layouts  12.6 us (6%)
  other arithmetic  11.9 us (6%)
    ppermute x2, waiting for transfers between devices, swapped(): return lax.ppermute(value, axis, pairs)  88.6 us
    all_to_all x1, waiting for transfers between devices, local(): lax.all_to_all(coeff_state.astype(jnp.float32), 'gy', split_axis=0, conca...  46.8 us
    dot_general x6, matrix products, local_pair_step(): jnp.einsum('gbck,kq->gbcq', joined, level_weights[half_bit], preferred_el...  13.7 us
    dot_general x2, matrix products, level_step(): jnp.einsum('bck,kq->bcq', joined, weight, preferred_element_type=jnp.floa...  9.31 us
    all_to_all x1, starting transfers between devices, local(): lax.all_to_all(later_angles, 'gy', split_axis=0, concat_axis=0, tiled=True)  6.35 us
    all_to_all x1, starting transfers between devices, local(): lax.all_to_all(coeff_state.astype(jnp.float32), 'gy', split_axis=0, conca...  5.09 us
    dot_general x1, matrix products, local(): jnp.einsum('ji,ick->jck', onehot, stacked, precision=lax.Precision.HIGHEST)  4.91 us
    another operation x4, other arithmetic  4.49 us
  transfers between devices with their start and end apart: 4, of which 3 were waited for; matrix products, arithmetic and copies ran while one was open for 8% of the time, Pallas kernels for 0%

commit v1 on v0

v1 whole, which is shorter than its diff:
```python
import functools

import jax
import jax.numpy as jnp
from jax import lax
from jax.experimental import pallas as pl
from jax.experimental.pallas import tpu as pltpu
from jax.sharding import PartitionSpec as P

SPLITS = 2


def level_plan(count_x, count_y):
    bits_x = count_x.bit_length() - 1
    bits_y = count_y.bit_length() - 1
    return [
        ("gy", bits_y - 1),
        ("gx", bits_x - 1),
        ("gy", bits_y - 2),
        ("gx", bits_x - 2),
        ("gy", bits_y - 3),
    ]


def kernel(
    count_x, count_y, per_peer, sides,
    inv_ref, src_ref, proj_ref, w_ref, cos0_ref, sin0_ref, ang_ref, interp_ref,
    out_ref,
    st0, got0, st1, got1, st2, got2, tmp_a, tmp_b, ang_got, cs, sn,
    a2a_send, a2a_recv, ang_send, ang_recv, ex_send, ex_recv,
):
    f32, bf16 = jnp.float32, jnp.bfloat16
    plan = level_plan(count_x, count_y)
    levels = len(plan)
    me_x = lax.axis_index("gx")
    me_y = lax.axis_index("gy")
    half = sides // SPLITS
    rows = 2 * half
    coeffs = st0.shape[-1]
    points = interp_ref.shape[1] // 2
    chunks = per_peer * SPLITS
    x_bits = [bit for axis, bit in plan if axis == "gx"]
    x_hbs = [(me_x // (1 << bit)) % 2 for bit in x_bits]
    partners = [me_x + (1 - 2 * hb) * (1 << bit) for hb, bit in zip(x_hbs, x_bits)]

    barrier = pltpu.get_barrier_semaphore()
    for k in range(1, count_y):
        pl.semaphore_signal(
            barrier, inc=1, device_id=(me_x, (me_y + k) % count_y),
            device_id_type=pl.DeviceIdType.MESH,
        )
    for partner in partners:
        pl.semaphore_signal(
            barrier, inc=1, device_id=(partner, me_y), device_id_type=pl.DeviceIdType.MESH
        )
    pl.semaphore_wait(barrier, count_y - 1 + len(partners))

    def ang_copy(k):
        peer = (me_y + k) % count_y
        return pltpu.make_async_remote_copy(
            src_ref=ang_ref.at[peer], dst_ref=ang_got.at[me_y],
            send_sem=ang_send.at[k], recv_sem=ang_recv.at[k],
            device_id=(me_x, peer), device_id_type=pl.DeviceIdType.MESH,
        )

    def a2a_copy(c, k):
        peer = (me_y + k) % count_y
        return pltpu.make_async_remote_copy(
            src_ref=st0.at[c, peer], dst_ref=got0.at[c, me_y],
            send_sem=a2a_send.at[c, k], recv_sem=a2a_recv.at[c, k],
            device_id=(me_x, peer), device_id_type=pl.DeviceIdType.MESH,
        )

    def swap_copy(which, c):
        source, target = ((st1, got1), (st2, got2))[which]
        return pltpu.make_async_remote_copy(
            src_ref=source.at[c], dst_ref=target.at[c],
            send_sem=ex_send.at[which, c], recv_sem=ex_recv.at[which, c],
            device_id=(partners[which], me_y), device_id_type=pl.DeviceIdType.MESH,
        )

    for k in range(1, count_y):
        ang_copy(k).start()
    ang_got[me_y] = ang_ref[me_y]

    def put(store, real, imag, cosine, sine):
        store(0, (cosine * real - sine * imag).astype(bf16))
        store(half, (sine * real + cosine * imag).astype(bf16))

    def project(c):
        r, q = c // SPLITS, c % SPLITS
        first = pl.multiple_of(q * half, half)
        group = jnp.concatenate(
            [src_ref[inv_ref[p * per_peer + r], pl.ds(first, half), :] for p in range(count_y)],
            axis=0,
        )
        prod = jnp.dot(group, proj_ref[...], preferred_element_type=f32)
        for p in range(count_y):
            block = prod[p * half : (p + 1) * half]

            def store(at, value, p=p):
                st0[c, p, at : at + half, :] = value

            slot = p * per_peer + r
            put(
                store, block[:, :coeffs], block[:, coeffs:],
                cos0_ref[pl.ds(slot, 1), :], sin0_ref[pl.ds(slot, 1), :],
            )

    def finish(prod, index, y, r, level, store):
        base = index * rows
        upper = prod[base : base + half]
        lower = prod[base + half : base + rows]
        real = upper[:, :coeffs] - lower[:, coeffs:]
        imag = lower[:, :coeffs] + upper[:, coeffs:]
        row = r * levels + level
        put(store, real, imag, cs[y, pl.ds(row, 1), :], sn[y, pl.ds(row, 1), :])

    def y_level(load, make_store, level, r):
        stride = 1 << plan[level][1]
        lows = [y for y in range(count_y) if (y // stride) % 2 == 0]
        low = jnp.concatenate([load(y) for y in lows], axis=0)
        high = jnp.concatenate([load(y + stride) for y in lows], axis=0)
        for h in range(2):
            prod = jnp.dot(low, w_ref[level, h, 0], preferred_element_type=f32)
            prod += jnp.dot(high, w_ref[level, h, 1], preferred_element_type=f32)
            for index, y in enumerate(lows):
                finish(prod, index, y + h * stride, r, level, make_store(y + h * stride))

    def x_level(mine, other, which, level, r, make_store):
        hb = x_hbs[which]
        prod = jnp.dot(mine, w_ref[level, hb, hb], preferred_element_type=f32)
        prod += jnp.dot(other, w_ref[level, hb, 1 - hb], preferred_element_type=f32)
        for y in range(count_y):
            finish(prod, y, y, r, level, make_store(y))

    def into(ref):
        def make_store(y):
            def store(at, value):
                ref[y, at : at + half, :] = value

            return store

        return make_store

    def into_chunk(ref, c):
        def make_store(y):
            def store(at, value):
                ref[c, y, at : at + half, :] = value

            return store

        return make_store

    def flat(value):
        return value.reshape(count_y * rows, coeffs)

    @pl.loop(0, chunks)
    def _(c):
        project(c)
        for k in range(1, count_y):
            a2a_copy(c, k).start()
        got0[c, me_y] = st0[c, me_y]

    for k in range(1, count_y):
        ang_copy(k).wait()
    for y in range(count_y):
        angle = ang_got[y]
        cs[y] = jnp.cos(angle)
        sn[y] = jnp.sin(angle)

    @pl.loop(0, chunks + 3)
    def _(t):
        @pl.when(t < chunks)
        def _():
            c = t
            for k in range(1, count_y):
                a2a_copy(c, k).wait()
            y_level(lambda y: got0[c, y], into_chunk(st1, c), 0, c // SPLITS)
            swap_copy(0, c).start()

        @pl.when((t >= 1) & (t < chunks + 1))
        def _():
            c = t - 1
            r = c // SPLITS
            swap_copy(0, c).wait()
            x_level(flat(st1[c]), flat(got1[c]), 0, 1, r, into(tmp_a))
            y_level(lambda y: tmp_a[y], into_chunk(st2, c), 2, r)
            swap_copy(1, c).start()

        @pl.when(t >= 3)
        def _():
            c = t - 3
            r, q = c // SPLITS, c % SPLITS
            swap_copy(1, c).wait()
            x_level(flat(st2[c]), flat(got2[c]), 1, 3, r, into(tmp_a))
            y_level(lambda y: tmp_a[y], into(tmp_b), 4, r)
            prod = jnp.dot(flat(tmp_b[...]), interp_ref[...], preferred_element_type=f32)
            first = pl.multiple_of(q * half, half)
            for y in range(count_y):
                upper = prod[y * rows : y * rows + half]
                lower = prod[y * rows + half : (y + 1) * rows]
                real = upper[:, :points] - lower[:, points:]
                imag = upper[:, points:] + lower[:, :points]
                out_ref[y * per_peer + r, pl.ds(first, half), :] = real.astype(bf16)
                out_ref[y * per_peer + r, pl.ds(first + sides, half), :] = imag.astype(bf16)


def local(sources, projection, translations, angles, interpolation, box_order):
    box_count, sides, points = sources.shape
    coeffs = projection.shape[1] // 2
    count_x, count_y = lax.axis_size("gx"), lax.axis_size("gy")
    per_peer = box_count // count_y
    levels = translations.shape[0]
    chunks = per_peer * SPLITS
    rows = 2 * sides // SPLITS
    slots = jnp.arange(box_count, dtype=jnp.int32)
    inverse = jnp.sum(
        jnp.where((box_order % box_count)[None, :] == slots[:, None], slots[None, :], 0), axis=1
    ).astype(jnp.int32)
    later = angles[1:].reshape(levels, count_y, per_peer, coeffs).transpose(1, 2, 0, 3)
    later = later.reshape(count_y, per_peer * levels, coeffs)
    weights = translations.reshape(levels, 2, 2, coeffs, 2 * coeffs)
    vmem = pl.BlockSpec(memory_space=pltpu.VMEM)
    state = pltpu.VMEM((chunks, count_y, rows, coeffs), jnp.bfloat16)
    single = pltpu.VMEM((count_y, rows, coeffs), jnp.bfloat16)
    phases = pltpu.VMEM((count_y, per_peer * levels, coeffs), jnp.float32)
    dma = pltpu.SemaphoreType.DMA
    return pl.pallas_call(
        functools.partial(kernel, count_x, count_y, per_peer, sides),
        out_shape=jax.ShapeDtypeStruct((box_count, 2 * sides, points), jnp.bfloat16),
        in_specs=[pl.BlockSpec(memory_space=pltpu.SMEM)] + [vmem] * 7,
        out_specs=vmem,
        scratch_shapes=[state] * 6 + [single] * 2 + [phases] * 3 + [
            dma((chunks, count_y)), dma((chunks, count_y)),
            dma((count_y,)), dma((count_y,)),
            dma((2, chunks)), dma((2, chunks)),
        ],
        compiler_params=pltpu.CompilerParams(
            collective_id=0, has_side_effects=True, vmem_limit_bytes=60 * 2**20
        ),
    )(
        inverse, sources, projection, weights, jnp.cos(angles[0]), jnp.sin(angles[0]),
        later, interpolation,
    )


def solution(mesh):
    placed = (
        P(("gx", "gy"), None, None),
        P(),
        P(),
        P(None, ("gx", "gy"), None),
        P(),
        P(("gx", "gy")),
    )
    return jax.shard_map(
        local, mesh=mesh, in_specs=placed, out_specs=P(("gx", "gy"), None, None), check_vma=False
    )
```

time: 208 us -> 101 us (0.49)
  waiting for transfers between devices: 135 us -> 0 us
  Pallas kernels: 0 us -> 91.8 us
  matrix products: 32.6 us -> 0 us
  starting transfers between devices: 14.5 us -> 0 us
  other arithmetic: 11.9 us -> 1.28 us
  local copies, waits for them, and re-layouts: 12.6 us -> 7.9 us
    pallas_call x0 -> x1, Pallas kernels: none -> 91.8 us  [local(): pl.pallas_call(functools.partial(kernel, count_x, count_y, per_peer, side...]
    ppermute x2 -> x0, waiting for transfers between devices: 88.6 us -> none  [swapped(): return lax.ppermute(value, axis, pairs)]
    all_to_all x2 -> x0, waiting for transfers between devices: 46.8 us -> none  [the longest x1 46.8 us: local(): lax.all_to_all(coeff_state.astype(jnp.float32), 'gy', split_axis=0, conca...]
    dot_general x11 -> x0, matrix products: 32.6 us -> none  [the longest x6 13.7 us: local_pair_step(): jnp.einsum('gbck,kq->gbcq', joined, level_weights[half_bit], preferred_el...]
    all_to_all x2 -> x0, starting transfers between devices: 11.4 us -> none  [the longest x1 6.35 us: local(): lax.all_to_all(later_angles, 'gy', split_axis=0, concat_axis=0, tiled=True)]
    concatenate x8 -> x0, other arithmetic: 5.8 us -> none  [the longest x6 2.97 us: rotate(): jnp.concatenate([cosine * real_part - sine_part * imag_part, sine_part *...]
    another operation x7 -> x0, other arithmetic: 4.97 us -> none
    slice x5 -> x1, local copies, waits for them, and re-layouts: 5.17 us -> 0.93 us  [local(): angles[1:].reshape(levels, count_y, per_peer, coeffs).transpose(1, 2, 0, 3)]
  transfers between devices with their start and end apart: 4 -> 0, of which waited for: 3 -> 0; matrix products, arithmetic and copies ran while one was open for 8% -> 0% of each run, Pallas kernels for 0% -> 0%
where the time goes in v1:
time: 101 us
  Pallas kernels  91.8 us (91%)
  local copies, waits for them, and re-layouts  7.9 us (8%)
  other arithmetic  1.28 us (1%)
    pallas_call x1, Pallas kernels, local(): pl.pallas_call(functools.partial(kernel, count_x, count_y, per_peer, side...  91.8 us
    unnamed x1, local copies, waits for them, and re-layouts  4.64 us

profile of v1, /device:TPU:0, one launch (start us, length us, event | category | flops | bytes accessed | tf_op | source)
XLA Modules:
  0.0 101.0 jit_solution(5874084626749009132)
XLA Ops:
  0.0 0.7 and_select_fusion
  0.7 0.6 select_reduce_fusion.inv_ref
  1.3 1.5 %sine_bitcast_fusion = (f32[32,256]{1,0:T(8,128)}, f32[32,256]{1,0:T(8,128)}) fusion(f32[6,32,256]{2,1,0:T(8,128)} %param.9), kind=kLoop, calls=%fused_computation | loop fusion | bytes 98304 | tf_op jit(solution)/shard_map/sin | solution.py:243
  2.8 0.9 slice.8
  3.8 0.7 copy.12.ang_ref
  4.6 91.8 %shard_map.64 = bf16[32,128,512]{2,1,0:T(8,128)(2,1)} custom-call(s32[32]{0:T(128)} %select_reduce_fusion.inv_ref, bf16[32,64,512]{2,1,0:T(8,128)(2,1)} %src_ref.1, bf16[512,512]{1,0:T(8,128)(2,1)} %proj_ref.1, bf16[5,2,2,256,512]{4,3,2,1,0:T(8,128)(2,1)} %bitcast.7, f32[32,256]{1,0:T(8,128)} %get-tuple-element.6.cos0_ref, ...), custom_call_target="tpu_custom_call" | custom-call | tf_op jit(solution)/shard_map/pallas_call | solution.py:229
  96.4 4.6 %copy.14 = bf16[32,128,512]{2,1,0:T(8,128)(2,1)} copy(bf16[32,128,512]{2,1,0:T(8,128)(2,1)} %shard_map.64) | data formatting | bytes 8388608
  (2 shorter events, 0.1 us)

commit v2 on v1

--- a/solution.py
+++ b/solution.py
@@ -8,6 +8,8 @@
 from jax.sharding import PartitionSpec as P
 
 SPLITS = 2
+LAG_X = 2
+LAG_END = 4
 
 
 def level_plan(count_x, count_y):
@@ -24,9 +26,9 @@
 
 def kernel(
     count_x, count_y, per_peer, sides,
-    inv_ref, src_ref, proj_ref, w_ref, cos0_ref, sin0_ref, ang_ref, interp_ref,
+    inv_ref, src_ref, proj_ref, w_ref, cos0_ref, sin0_ref, ang_ref,
     out_ref,
-    st0, got0, st1, got1, st2, got2, tmp_a, tmp_b, ang_got, cs, sn,
+    st0, got0, st1, got1, st2, got2, tmp_a, wx, ang_got, cs, sn,
     a2a_send, a2a_recv, ang_send, ang_recv, ex_send, ex_recv,
 ):
     f32, bf16 = jnp.float32, jnp.bfloat16
@@ -37,9 +39,9 @@
     half = sides // SPLITS
     rows = 2 * half
     coeffs = st0.shape[-1]
-    points = interp_ref.shape[1] // 2
     chunks = per_peer * SPLITS
     x_bits = [bit for axis, bit in plan if axis == "gx"]
+    x_levels = [level for level, (axis, bit) in enumerate(plan) if axis == "gx"]
     x_hbs = [(me_x // (1 << bit)) % 2 for bit in x_bits]
     partners = [me_x + (1 - 2 * hb) * (1 << bit) for hb, bit in zip(x_hbs, x_bits)]
 
@@ -82,6 +84,12 @@
     for k in range(1, count_y):
         ang_copy(k).start()
     ang_got[me_y] = ang_ref[me_y]
+
+    for which, (level, hb) in enumerate(zip(x_levels, x_hbs)):
+        own = pl.multiple_of(hb * coeffs, coeffs)
+        rest = pl.multiple_of((1 - hb) * coeffs, coeffs)
+        wx[which, :coeffs, :] = w_ref[level, hb, pl.ds(own, coeffs), :]
+        wx[which, coeffs:, :] = w_ref[level, hb, pl.ds(rest, coeffs), :]
 
     def put(store, real, imag, cosine, sine):
         store(0, (cosine * real - sine * imag).astype(bf16))
@@ -121,18 +129,17 @@
         lows = [y for y in range(count_y) if (y // stride) % 2 == 0]
         low = jnp.concatenate([load(y) for y in lows], axis=0)
         high = jnp.concatenate([load(y + stride) for y in lows], axis=0)
+        joined = jnp.concatenate([low, high], axis=1)
         for h in range(2):
-            prod = jnp.dot(low, w_ref[level, h, 0], preferred_element_type=f32)
-            prod += jnp.dot(high, w_ref[level, h, 1], preferred_element_type=f32)
+            prod = jnp.dot(joined, w_ref[level, h], preferred_element_type=f32)
             for index, y in enumerate(lows):
                 finish(prod, index, y + h * stride, r, level, make_store(y + h * stride))
 
-    def x_level(mine, other, which, level, r, make_store):
-        hb = x_hbs[which]
-        prod = jnp.dot(mine, w_ref[level, hb, hb], preferred_element_type=f32)
-        prod += jnp.dot(other, w_ref[level, hb, 1 - hb], preferred_element_type=f32)
+    def x_level(mine, other, which, r, make_store):
+        joined = jnp.concatenate([mine, other], axis=1)
+        prod = jnp.dot(joined, wx[which], preferred_element_type=f32)
         for y in range(count_y):
-            finish(prod, y, y, r, level, make_store(y))
+            finish(prod, y, y, r, x_levels[which], make_store(y))
 
     def into(ref):
         def make_store(y):
@@ -169,7 +176,7 @@
         cs[y] = jnp.cos(angle)
         sn[y] = jnp.sin(angle)
 
-    @pl.loop(0, chunks + 3)
+    @pl.loop(0, chunks + LAG_END)
     def _(t):
         @pl.when(t < chunks)
         def _():
@@ -179,31 +186,47 @@
             y_level(lambda y: got0[c, y], into_chunk(st1, c), 0, c // SPLITS)
             swap_copy(0, c).start()
 
-        @pl.when((t >= 1) & (t < chunks + 1))
+        @pl.when((t >= LAG_X) & (t < chunks + LAG_X))
         def _():
-            c = t - 1
+            c = t - LAG_X
             r = c // SPLITS
             swap_copy(0, c).wait()
-            x_level(flat(st1[c]), flat(got1[c]), 0, 1, r, into(tmp_a))
+            x_level(flat(st1[c]), flat(got1[c]), 0, r, into(tmp_a))
             y_level(lambda y: tmp_a[y], into_chunk(st2, c), 2, r)
             swap_copy(1, c).start()
 
-        @pl.when(t >= 3)
+        @pl.when(t >= LAG_END)
         def _():
-            c = t - 3
+            c = t - LAG_END
             r, q = c // SPLITS, c % SPLITS
             swap_copy(1, c).wait()
-            x_level(flat(st2[c]), flat(got2[c]), 1, 3, r, into(tmp_a))
-            y_level(lambda y: tmp_a[y], into(tmp_b), 4, r)
-            prod = jnp.dot(flat(tmp_b[...]), interp_ref[...], preferred_element_type=f32)
+            x_level(flat(st2[c]), flat(got2[c]), 1, r, into(tmp_a))
             first = pl.multiple_of(q * half, half)
-            for y in range(count_y):
-                upper = prod[y * rows : y * rows + half]
-                lower = prod[y * rows + half : (y + 1) * rows]
-                real = upper[:, :points] - lower[:, points:]
-                imag = upper[:, points:] + lower[:, :points]
-                out_ref[y * per_peer + r, pl.ds(first, half), :] = real.astype(bf16)
-                out_ref[y * per_peer + r, pl.ds(first + sides, half), :] = imag.astype(bf16)
+
+            def make_store(y):
+                def store(at, value):
+                    begin = first if at == 0 else first + sides
+                    out_ref[y * per_peer + r, pl.ds(begin, half), :] = value
+
+                return store
+
+            y_level(lambda y: tmp_a[y], make_store, 4, r)
+
+
+def interpolate_kernel(state_ref, interp_ref, out_ref):
+    group, rows, coeffs = state_ref.shape
+    sides, points = rows // 2, interp_ref.shape[1] // 2
+    prod = jnp.dot(
+        state_ref[...].reshape(group * rows, coeffs), interp_ref[...],
+        preferred_element_type=jnp.float32,
+    )
+    for g in range(group):
+        upper = prod[g * rows : g * rows + sides]
+        lower = prod[g * rows + sides : (g + 1) * rows]
+        real = upper[:, :points] - lower[:, points:]
+        imag = upper[:, points:] + lower[:, :points]
+        out_ref[g, :sides, :] = real.astype(out_ref.dtype)
+        out_ref[g, sides:, :] = imag.astype(out_ref.dtype)
 
 
 def local(sources, projection, translations, angles, interpolation, box_order):
@@ -220,18 +243,17 @@
     ).astype(jnp.int32)
     later = angles[1:].reshape(levels, count_y, per_peer, coeffs).transpose(1, 2, 0, 3)
     later = later.reshape(count_y, per_peer * levels, coeffs)
-    weights = translations.reshape(levels, 2, 2, coeffs, 2 * coeffs)
     vmem = pl.BlockSpec(memory_space=pltpu.VMEM)
     state = pltpu.VMEM((chunks, count_y, rows, coeffs), jnp.bfloat16)
     single = pltpu.VMEM((count_y, rows, coeffs), jnp.bfloat16)
     phases = pltpu.VMEM((count_y, per_peer * levels, coeffs), jnp.float32)
     dma = pltpu.SemaphoreType.DMA
-    return pl.pallas_call(
+    state_out = pl.pallas_call(
         functools.partial(kernel, count_x, count_y, per_peer, sides),
-        out_shape=jax.ShapeDtypeStruct((box_count, 2 * sides, points), jnp.bfloat16),
-        in_specs=[pl.BlockSpec(memory_space=pltpu.SMEM)] + [vmem] * 7,
+        out_shape=jax.ShapeDtypeStruct((box_count, 2 * sides, coeffs), jnp.bfloat16),
+        in_specs=[pl.BlockSpec(memory_space=pltpu.SMEM)] + [vmem] * 6,
         out_specs=vmem,
-        scratch_shapes=[state] * 6 + [single] * 2 + [phases] * 3 + [
+        scratch_shapes=[state] * 6 + [single] + [pltpu.VMEM((2, 2 * coeffs, 2 * coeffs), jnp.bfloat16)] + [phases] * 3 + [
             dma((chunks, count_y)), dma((chunks, count_y)),
             dma((count_y,)), dma((count_y,)),
             dma((2, chunks)), dma((2, chunks)),
@@ -240,9 +262,20 @@
             collective_id=0, has_side_effects=True, vmem_limit_bytes=60 * 2**20
         ),
     )(
-        inverse, sources, projection, weights, jnp.cos(angles[0]), jnp.sin(angles[0]),
-        later, interpolation,
-    )
+        inverse, sources, projection, translations, jnp.cos(angles[0]), jnp.sin(angles[0]),
+        later,
+    )
+    group = 4
+    return pl.pallas_call(
+        interpolate_kernel,
+        out_shape=jax.ShapeDtypeStruct((box_count, 2 * sides, points), jnp.bfloat16),
+        grid=(box_count // group,),
+        in_specs=[
+            pl.BlockSpec((group, 2 * sides, coeffs), lambda i: (i, 0, 0)),
+            pl.BlockSpec(interpolation.shape, lambda i: (0, 0)),
+        ],
+        out_specs=pl.BlockSpec((group, 2 * sides, points), lambda i: (i, 0, 0)),
+    )(state_out, interpolation)
 
 
 def solution(mesh):

time: 101 us -> 107 us (1.059)
  Pallas kernels: 91.8 us -> 101 us
  local copies, waits for them, and re-layouts: 7.9 us -> 3.25 us
    pallas_call x0 -> x1, Pallas kernels: none -> 7.79 us  [local(): pl.pallas_call(interpolate_kernel, out_shape=jax.ShapeDtypeStruct((box_co...]
    unnamed x1 -> x0, local copies, waits for them, and re-layouts: 4.64 us -> none
    pallas_call x1, Pallas kernels: 91.8 us -> 93.6 us  [local(): pl.pallas_call(functools.partial(kernel, count_x, count_y, per_peer, side...]
where the time goes in v2:
time: 107 us; the launch traced here: 106 us
  Pallas kernels  101 us (94%)
  local copies, waits for them, and re-layouts  3.25 us (3%)
  other arithmetic  1.34 us (1%)
    pallas_call x1, Pallas kernels, local(): pl.pallas_call(functools.partial(kernel, count_x, count_y, per_peer, side...  93.6 us
    pallas_call x1, Pallas kernels, local(): pl.pallas_call(interpolate_kernel, out_shape=jax.ShapeDtypeStruct((box_co...  7.79 us

profile of v2, /device:TPU:0, one launch (start us, length us, event | category | flops | bytes accessed | tf_op | source)
XLA Modules:
  0.0 106.0 jit_solution(7146058473838001883)
XLA Ops:
  0.0 0.7 and_select_fusion
  0.7 0.7 select_reduce_fusion.inv_ref
  1.3 1.5 %sine_bitcast_fusion = (f32[32,256]{1,0:T(8,128)}, f32[32,256]{1,0:T(8,128)}) fusion(f32[6,32,256]{2,1,0:T(8,128)} %param.9), kind=kLoop, calls=%fused_computation | loop fusion | bytes 98304 | tf_op jit(solution)/shard_map/sin | solution.py:265
  2.9 0.9 slice.8
  3.9 0.7 copy.12.ang_ref
  4.6 93.6 %shard_map.64.state_ref = bf16[32,128,256]{2,1,0:T(8,128)(2,1)} custom-call(s32[32]{0:T(128)} %select_reduce_fusion.inv_ref, bf16[32,64,512]{2,1,0:T(8,128)(2,1)} %src_ref.1, bf16[512,512]{1,0:T(8,128)(2,1)} %proj_ref.1, bf16[5,2,512,512]{3,2,1,0:T(8,128)(2,1)} %w_ref.1, f32[32,256]{1,0:T(8,128)} %get-tuple-element.6.cos0_ref, ...), custom_call_target="tpu_custom_call" | custom-call | tf_op jit(solution)/shard_map/pallas_call | solution.py:251
  98.2 7.8 %shard_map.65 = bf16[32,128,512]{2,1,0:T(8,128)(2,1)} custom-call(bf16[32,128,256]{2,1,0:T(8,128)(2,1)} %shard_map.64.state_ref, bf16[256,1024]{1,0:T(8,128)(2,1)} %interp_ref.1), custom_call_target="tpu_custom_call" | custom-call | tf_op jit(solution)/shard_map/pallas_call | solution.py:269
  (2 shorter events, 0.1 us)
